TPU v7x, 256 devices: a whole 4x4x8 slice. The times are simulated.
256 devices in a mesh: gx: 8 (over x, core), gy: 8 (over z), wa: 4 (over y).
Axes of the slice: x: 4, y: 4, z: 8, core: 2. Of those that a mesh axis runs over, the one named last changes fastest.
Arguments:
- velocity: float32 [3, 256, 512, 512], P(None, 'gx', 'gy', 'wa'), may hold values from -70 to 70, as said below
- lengths: int32 [8, 8, 4, 2048], P('gx', 'gy', 'wa'), may hold values from 16 to 128
- destinations: int32 [8, 8, 4, 2048, 1], P('gx', 'gy', 'wa'), may hold values from 0 to 63; in each aligned block of 2048 rows (0 to 2047, 2048 to 4095, ..., all dimensions but the last counted through in order) at most 64 rows name the same one
Outputs:
- received: float32 [64, 4, 3, 64, 64, 128], P(('gx', 'gy'), 'wa')
Inputs may be any that keep to these rules, and one draw needn't show every extreme that they name: `velocity`: finite values; the amplitude varies over the grid. `destinations`: in every draw no device sends more than 64 blocks to one writer, and some device sends exactly 64 to one writer.
All inputs are finite; a program needn't handle non-finite values.
Results may differ from a plain program's by a relative error of at most 0.0003.
Values sent between devices are 32-bit elements; how exact they have to be, the bound alone decides.
A program may use at most 128 MiB of HBM per device.

v0:
```python
import jax
import jax.numpy as jnp
from jax import lax
from jax.sharding import Mesh
from jax.sharding import PartitionSpec as P

BY = 8
BZ = 16
GX_GY_WA = ("gx_0", "gx_1", "gy", "wa")
GX = ("gx_0", "gx_1")
GX_GY = ("gx_0", "gx_1", "gy")


def extended(array, sides, width):
    for axis, dim in sides:
        peers, length = (lax.axis_size(axis), array.shape[dim])
        up = [(i, (i + 1) % peers) for i in range(peers)]
        down = [(j, i) for i, j in up]
        last = lax.slice_in_dim(array, length - width, length, axis=dim)
        leading = lax.slice_in_dim(array, 0, width, axis=dim)
        before = lax.ppermute(last, axis, up)
        after = lax.ppermute(leading, axis, down)
        array = jnp.concatenate([before, array, after], axis=dim)
    return array


def over_axes(array, axes):
    for axis in axes:
        array = lax.psum(array, axis)
    return array


def dct_table(count):
    freqs = jnp.arange(count, dtype=jnp.float32)[:, None]
    points = jnp.arange(count, dtype=jnp.float32)[None, :]
    table = jnp.cos(jnp.pi * (points + 0.5) * freqs / count) * jnp.sqrt(2.0 / count)
    return jnp.where(freqs == 0.0, table * jnp.sqrt(0.5), table)


def curl_field(padded):

    def along_x(component):
        return (padded[component, 2:, 1:-1, 1:-1] - padded[component, :-2, 1:-1, 1:-1]) * 0.5

    def along_y(component):
        return (padded[component, 1:-1, 2:, 1:-1] - padded[component, 1:-1, :-2, 1:-1]) * 0.5

    def along_z(component):
        return (padded[component, 1:-1, 1:-1, 2:] - padded[component, 1:-1, 1:-1, :-2]) * 0.5

    first = along_y(2) - along_z(1)
    second = along_z(0) - along_x(2)
    third = along_x(1) - along_y(0)
    return jnp.stack([first, second, third])


def transform(curl):
    comps, cells_x, cells_y, cells_z = curl.shape
    kron_table = jnp.kron(dct_table(BY), dct_table(BZ)).T.reshape(BY, BZ, BY * BZ)
    grouped = curl.reshape(comps, cells_x, cells_y // BY, BY, cells_z // BZ, BZ)
    coeffs = lax.dot_general(
        grouped,
        kron_table,
        (((3, 5), (0, 1)), ((), ())),
        precision=lax.Precision.HIGHEST,
        preferred_element_type=jnp.float32,
    )
    return coeffs.reshape(comps, -1, BY * BZ)


def local(velocity, lengths, destinations):
    padded = extended(velocity, ((GX, 1), ("gy", 2), ("wa", 3)), 1)
    curl = curl_field(padded)
    coeffs = transform(curl)
    total = over_axes(jnp.sum(coeffs * coeffs), GX_GY_WA)
    every = curl.size * lax.axis_size(GX) * lax.axis_size("gy") * lax.axis_size("wa")
    rms = jnp.sqrt(total / every + 1e-06)
    comps, nblk, width = coeffs.shape
    rows_x = lax.axis_size(GX)
    rows_y = lax.axis_size("gy")
    writer_count = rows_x * rows_y
    capacity = max(2, 2 * nblk // writer_count)
    targets = destinations.reshape(nblk)
    lens = lengths.reshape(nblk)
    onehot = (targets[:, None] == jnp.arange(writer_count, dtype=jnp.int32)[None, :]).astype(
        jnp.int32
    )
    before = jnp.cumsum(onehot, axis=0) - onehot
    ranking = jnp.sum(before * onehot, axis=1)
    slot_index = targets * capacity + ranking
    source = jnp.full((writer_count * capacity,), -1, jnp.int32)
    source = source.at[slot_index].set(jnp.arange(nblk, dtype=jnp.int32))
    present = source >= 0
    safe = jnp.maximum(source, 0)
    picked = jnp.take(coeffs, safe, axis=1)
    freqs = jnp.arange(width, dtype=jnp.int32)
    keep = (freqs[None, :] < jnp.take(lens, safe)[:, None]) & present[:, None]
    outgoing = jnp.where(keep[None, :, :], picked / rms, 0.0)
    outgoing = outgoing.reshape(comps, writer_count, capacity, width)
    arrived = lax.all_to_all(outgoing, GX_GY, split_axis=1, concat_axis=1, tiled=True)
    return arrived.reshape(1, 1, comps, writer_count, capacity, width)


def solution(mesh):
    finer = Mesh(
        mesh.devices.reshape(4, 2, mesh.shape["gy"], mesh.shape["wa"]), ("gx_0", "gx_1", "gy", "wa")
    )
    return jax.shard_map(
        local,
        mesh=finer,
        in_specs=(P(None, GX, "gy", "wa"), P(GX, "gy", "wa", None), P(GX, "gy", "wa", None, None)),
        out_specs=P(GX_GY, "wa", None, None, None, None),
        check_vma=False,
    )
```

profile of v0, /device:TPU:1, one launch (start us, length us, event | category | flops | bytes accessed | tf_op | source)
XLA Modules:
  0.0 446.5 jit_solution(11419711120034385909)
XLA Ops:
  0.0 1.0 fusion.18
  1.0 2.6 collective-permute-start
  3.6 0.6 collective-permute-start.1
  4.3 0.7 fusion.11
  5.0 18.1 %reduce-window.6 = s32[64,16,128]{2,1,0:T(8,128)S(1)} reduce-window(s32[64,16,128]{2,1,0:T(8,128)S(1)} %fusion.11, s32[]{:T(128)} %constant.25.clone.1), window={size=1x1x128 pad=0_0x0_0x127_0}, to_apply=%region_0.1 | reduce-window | flops 16646144 | bytes 1048580 | tf_op jit(solution)/shard_map/reduce-window
  23.1 0.2 slice.96
  23.4 0.4 copy.38
  23.8 0.2 reduce-window.9
  24.0 0.2 broadcast_add_fusion
  24.2 0.3 fusion.10
  24.5 8.1 %scatter_custom_fusion = s32[4096]{0:T(1024)S(1)} fusion(s32[2048]{0:T(1024)S(1)} %bitcast.68, s32[2048]{0:T(1024)S(1)} %iota.50, s32[]{:T(128)} %constant.22.clone.1), kind=kCustom, calls=%fused_computation.48 | custom fusion | bytes 16388 | tf_op jit(solution)/shard_map/scatter | solution.py:92
  32.6 23.0 %gather_fusion = s32[4096]{0:T(1024)S(1)} fusion(s32[2048]{0:T(1024)S(1)} %bitcast.54, s32[4096]{0:T(1024)S(1)} %maximum_clamp_fusion), kind=kCustom, calls=%fused_computation | custom fusion | bytes 49152 | tf_op jit(solution)/shard_map/jit(_take)/gather | solution.py:97
  56.0 2.3 fusion.7
  58.5 0.2 mul.189
  58.7 0.9 constant_dynamic-update-slice_fusion.6
  59.6 2.8 constant_dynamic-update-slice_fusion.5
  62.5 0.9 constant_dynamic-update-slice_fusion.3
  63.4 0.7 fusion.15
  64.1 5.0 %collective-permute-start.2 = (f32[3,34,1,128]{3,2,1,0:T(1,128)}, f32[3,34,1,128]{3,2,1,0:T(1,128)S(1)}, u32[]{:S(2)}, u32[]{:S(2)}) collective-permute-start(f32[3,34,1,128]{3,2,1,0:T(1,128)} %get-tuple-element.18), channel_id=1, source_target_pairs={{4,0},{8,4},{12,8},{16,12},{20,16},{24,20},{28,24},{0,28},{5,1},{9... | collective-permute-start | bytes 156680 | tf_op jit(solution)/shard_map/ppermute | solution.py:22
  69.0 1.5 fusion.17
  70.6 1.5 fusion.16
  72.0 3.6 copy.41
  75.6 3.7 copy.42
  79.3 3.7 copy.43
  83.0 3.8 copy.44
  86.8 2.5 pad_maximum_fusion.2
  89.3 10.2 %copy.23 = f32[3,34,66,128]{1,3,2,0:T(8,128)} copy(f32[3,34,66,128]{3,2,1,0:T(8,128)} %pad_maximum_fusion.2) | data formatting | bytes 6893568 | tf_op jit(solution)/shard_map/concatenate | solution.py:23
  99.4 2.2 fusion.14
  101.7 2.7 collective-permute-start.4
  104.4 2.3 pad_maximum_fusion.5
  106.7 3.8 copy.45
  110.4 2.7 copy.46
  113.1 10.3 %multiply_subtract_fusion = f32[1,32,64,128]{1,3,2,0:T(8,128)} fusion(f32[1,32,64,128]{1,3,2,0:T(8,128)} %copy.45, f32[1,32,64,128]{1,3,2,0:T(8,128)} %copy.46, f32[1,32,64,128]{1,3,2,0:T(8,128)} %copy.43, f32[1,32,64,128]{1,3,2,0:T(8,128)} %copy.44), kind=kLoop, calls=%fused_computation.15 | loop fusion | flops 1310720 | bytes 5242880 | tf_op jit(solution)/shard_map/sub | solution.py:53
  123.4 2.7 copy.39
  126.2 2.8 copy.40
  129.0 18.5 %fusion.6 = (f32[1,32,64,128]{1,3,2,0:T(8,128)}, f32[1,32,64,128]{1,3,2,0:T(8,128)}) fusion(f32[3,34,66,128]{1,3,2,0:T(8,128)} %copy.23, f32[3,34,66,1]{1,3,2,0:T(1,128)} %collective-permute-done.5, f32[3,34,66,1]{1,3,2,0:T(1,128)} %collective-permute-done.4, f32[1,32,64,128]{1,3,2,0:T(8,128)} %copy.39, f32[1,32,64,128]{1,3,2,0:T(8,128)} %copy.40, ...), kind=kLoop, calls=%fused_computation.14 | loop fusion | flops 3670016 | bytes 9792096 | tf_op jit(solution)/shard_map/sub | solution.py:51
  147.5 10.3 %maximum_bitcast_fusion = f32[3,32,8,8,8,16]{1,5,3,4,2,0:T(8,128)} fusion(f32[1,32,8,8,8,16]{1,5,4,3,2,0:T(8,128)S(1)} %bitcast.58, f32[1,32,8,8,8,16]{1,5,4,3,2,0:T(8,128)} %bitcast.60, f32[1,32,8,8,8,16]{1,5,4,3,2,0:T(8,128)} %bitcast.59), kind=kLoop, calls=%fused_computation.3 | loop fusion | flops 1572864 | bytes 6291456 | tf_op jit(solution)/shard_map/dot_general | solution.py:61
  157.8 23.1 %copy.47 = f32[3,32,8,8,8,16]{5,3,2,1,4,0:T(8,128)} copy(f32[3,32,8,8,8,16]{1,5,3,4,2,0:T(8,128)} %maximum_bitcast_fusion) | data formatting | bytes 6291456 | tf_op jit(solution)/shard_map/dot_general | solution.py:61
  180.9 24.0 %multiply_reduce_fusion = (f32[]{:T(128)}, f32[3,2048,128]{2,1,0:T(8,128)S(1)}) fusion(f32[3,2048,8,16]{3,1,2,0:T(8,128)} %bitcast.55, f32[8,16,128,1]{2,1,0,3:T(8,128)S(1)} %bitcast.62), kind=kOutput, calls=%fused_computation.17 | convolution fusion | flops 1209532416 | bytes 6356996 | tf_op jit(solution)/shard_map/dot_general | solution.py:61
  204.9 8.1 %psum.28 = f32[]{:T(128)} all-reduce(f32[]{:T(128)} %get-tuple-element.32), channel_id=1, replica_groups=mesh['gx_0'=4,'gx_1'=2,'gy'=8,'wa'=4] {'gx_0'}, use_global_device_ids=true, to_apply=%region_5.6 | all-reduce | flops 1 | bytes 8 | tf_op jit(solution)/shard_map/psum | solution.py:29
  213.0 7.0 %psum.29 = f32[]{:T(128)} all-reduce(f32[]{:T(128)} %psum.28), channel_id=1, replica_groups=mesh['gx_0'=4,'gx_1'=2,'gy'=8,'wa'=4] {'gx_1'}, use_global_device_ids=true, to_apply=%region_6.7 | all-reduce | flops 1 | bytes 8 | tf_op jit(solution)/shard_map/psum | solution.py:29
  220.0 10.0 %copy.34 = f32[3,2048,128]{2,0,1:T(4,128)} copy(f32[3,2048,128]{2,1,0:T(8,128)S(1)} %get-tuple-element.33) | data formatting | bytes 6291456 | tf_op jit(solution)/shard_map/dot_general | solution.py:61
  229.9 14.2 %psum.30 = f32[]{:T(128)} all-reduce(f32[]{:T(128)} %psum.29), channel_id=1, replica_groups=mesh['gx_0'=4,'gx_1'=2,'gy'=8,'wa'=4] {'gy'}, use_global_device_ids=true, to_apply=%region_7.8 | all-reduce | flops 1 | bytes 8 | tf_op jit(solution)/shard_map/psum | solution.py:29
  244.2 32.5 %gather_fusion.1 = f32[4096,3,128]{2,1,0:T(4,128)} fusion(f32[3,2048,128]{2,0,1:T(4,128)} %copy.34, s32[4096]{0:T(1024)S(1)} %maximum_clamp_fusion), kind=kCustom, calls=%fused_computation.1 | custom fusion | bytes 12599296 | tf_op jit(solution)/shard_map/jit(_take)/gather | solution.py:95
  276.7 9.5 %psum.31 = f32[]{:T(128)} all-reduce(f32[]{:T(128)} %psum.30), channel_id=1, replica_groups=mesh['gx_0'=4,'gx_1'=2,'gy'=8,'wa'=4] {'wa'}, use_global_device_ids=true, to_apply=%region_8.9 | all-reduce | flops 1 | bytes 8 | tf_op jit(solution)/shard_map/psum | solution.py:29
  286.9 5.0 %fusion.1 = f32[3,64,64,128]{3,2,0,1:T(8,128)S(1)} fusion(f32[3,64,64,128]{3,0,2,1:T(4,128)} %bitcast.56, f32[]{:T(128)S(6)} %sqrt.3, pred[64,64]{1,0:T(8,128)(4,1)S(1)} %broadcast_in_dim.69, pred[64,64,128]{2,1,0:T(8,128)(4,1)S(1)} %copy-done.6), kind=kLoop, calls=%fused_computation.6 | loop fusion | flops 4718592 | bytes 13111300 | tf_op jit(solution)/shard_map/jit(_where)/select_n | solution.py:98
  291.9 151.2 %all_to_all.5 = f32[3,64,64,128]{3,2,0,1:T(8,128)S(1)} all-to-all(f32[3,64,64,128]{3,2,0,1:T(8,128)S(1)} %fusion.1), channel_id=1, replica_groups=mesh['gx_0'=4,'gx_1'=2,'gy'=8,'wa'=4] {'gx_0','gx_1','gy'}, dimensions={1} | all-to-all | bytes 12582912 | tf_op jit(solution)/shard_map/all_to_all | solution.py:100
  443.2 3.3 copy.36
  (39 shorter events, 0.7 us)
Async XLA Ops:
  0.0 32.6 %copy-start = (s32[1,1,1,2048]{3,2,1,0:T(1,128)S(1)}, s32[1,1,1,2048]{3,2,1,0:T(1,128)}, u32[]{:S(2)}) copy-start(s32[1,1,1,2048]{3,2,1,0:T(1,128)} %param.4) | copy-start | bytes 24580
  0.0 24.2 %copy-start.7 = (s32[1,1,1,2048,1]{3,4,2,1,0:T(1,128)S(1)}, s32[1,1,1,2048,1]{3,4,2,1,0:T(1,128)}, u32[]{:S(2)}) copy-start(s32[1,1,1,2048,1]{3,4,2,1,0:T(1,128)} %param.5) | copy-start | bytes 24580
  1.0 57.7 %collective-permute-start = (f32[3,1,64,128]{3,2,1,0:T(8,128)S(1)}, f32[3,1,64,128]{3,2,1,0:T(8,128)}, u32[]{:S(2)}, u32[]{:S(2)}) collective-permute-start(f32[3,1,64,128]{3,2,1,0:T(8,128)S(1)} %get-tuple-element.27), channel_id=1, source_target_pairs={{0,32},{32,64},{64,96},{96,128},{128,160},{160,192},{192,224},{224... | collective-permute-start | bytes 294920 | tf_op jit(solution)/shard_map/ppermute | solution.py:21
  3.6 58.9 %collective-permute-start.1 = (f32[3,1,64,128]{3,2,1,0:T(8,128)S(1)}, f32[3,1,64,128]{3,2,1,0:T(8,128)}, u32[]{:S(2)}, u32[]{:S(2)}) collective-permute-start(f32[3,1,64,128]{3,2,1,0:T(8,128)S(1)} %get-tuple-element.26), channel_id=1, source_target_pairs={{32,0},{64,32},{96,64},{128,96},{160,128},{192,160},{224,192},{0,2... | collective-permute-start | bytes 294920 | tf_op jit(solution)/shard_map/ppermute | solution.py:22
  64.1 22.7 %collective-permute-start.2 = (f32[3,34,1,128]{3,2,1,0:T(1,128)}, f32[3,34,1,128]{3,2,1,0:T(1,128)S(1)}, u32[]{:S(2)}, u32[]{:S(2)}) collective-permute-start(f32[3,34,1,128]{3,2,1,0:T(1,128)} %get-tuple-element.18), channel_id=1, source_target_pairs={{4,0},{8,4},{12,8},{16,12},{20,16},{24,20},{28,24},{0,28},{5,1},{9... | collective-permute-start | bytes 156680 | tf_op jit(solution)/shard_map/ppermute | solution.py:22
  69.0 17.8 %collective-permute-start.3 = (f32[3,34,1,128]{3,2,1,0:T(1,128)}, f32[3,34,1,128]{3,2,1,0:T(1,128)S(1)}, u32[]{:S(2)}, u32[]{:S(2)}) collective-permute-start(f32[3,34,1,128]{3,2,1,0:T(1,128)} %get-tuple-element.17), channel_id=1, source_target_pairs={{0,4},{4,8},{8,12},{12,16},{16,20},{20,24},{24,28},{28,0},{1,5},{5... | collective-permute-start | bytes 156680 | tf_op jit(solution)/shard_map/ppermute | solution.py:21
  101.7 27.3 %collective-permute-start.4 = (f32[3,34,66,1]{1,3,2,0:T(1,128)}, f32[3,34,66,1]{1,3,2,0:T(1,128)}, u32[]{:S(2)}, u32[]{:S(2)}) collective-permute-start(f32[3,34,66,1]{1,3,2,0:T(1,128)} %get-tuple-element.9), channel_id=1, source_target_pairs={{1,0},{2,1},{3,2},{0,3},{5,4},{6,5},{7,6},{4,7},{9,8},{10,9},{11,1... | collective-permute-start | bytes 80792 | tf_op jit(solution)/shard_map/ppermute | solution.py:22
  104.4 24.6 %collective-permute-start.5 = (f32[3,34,66,1]{1,3,2,0:T(1,128)}, f32[3,34,66,1]{1,3,2,0:T(1,128)}, u32[]{:S(2)}, u32[]{:S(2)}) collective-permute-start(f32[3,34,66,1]{1,3,2,0:T(1,128)} %get-tuple-element.10), channel_id=1, source_target_pairs={{0,1},{1,2},{2,3},{3,0},{4,5},{5,6},{6,7},{7,4},{8,9},{9,10},{10,1... | collective-permute-start | bytes 80792 | tf_op jit(solution)/shard_map/ppermute | solution.py:21
  106.7 3.8 copy-start.5
  113.1 10.3 %copy-start.4 = (f32[1,32,64,128]{3,2,1,0:T(8,128)S(1)}, f32[1,32,64,128]{3,2,1,0:T(8,128)}, u32[]{:S(2)}) copy-start(f32[1,32,64,128]{3,2,1,0:T(8,128)} %get-tuple-element.16) | copy-start | bytes 3145732
  123.4 2.7 copy-start.3
  129.0 18.5 %copy-start.2 = (f32[1,32,64,128]{1,3,2,0:T(8,128)S(1)}, f32[1,32,64,128]{1,3,2,0:T(8,128)}, u32[]{:S(2)}) copy-start(f32[1,32,64,128]{1,3,2,0:T(8,128)} %multiply_subtract_fusion) | copy-start | bytes 3145732
  244.2 42.7 %copy-start.6 = (pred[64,64,128]{2,1,0:T(8,128)(4,1)S(1)}, pred[64,64,128]{2,1,0:T(8,128)(4,1)}, u32[]{:S(2)}) copy-start(pred[64,64,128]{2,1,0:T(8,128)(4,1)} %fusion.7) | copy-start | bytes 1572868
  443.2 3.3 copy-start.1
where the time goes:
time: 448 us; the launch traced here: 446 us
  blocking collectives  190 us (42%)
  local copies, waits for them, and re-layouts  149 us (33%)
  other arithmetic  71.2 us (16%)
  matrix products  24 us (5%)
  starting transfers between devices  10.9 us (2%)
    all_to_all x1, blocking collectives, local(): lax.all_to_all(outgoing, GX_GY, split_axis=1, concat_axis=1, tiled=True)  151 us
    psum x4, blocking collectives, over_axes(): array = lax.psum(array, axis)  38.8 us
    dot_general x2, local copies, waits for them, and re-layouts, transform(): lax.dot_general(grouped, kron_table, (((3, 5), (0, 1)), ((), ())), precis...  33 us
    gather x1, local copies, waits for them, and re-layouts, local(): picked = jnp.take(coeffs, safe, axis=1)  32.5 us
    unnamed x25, local copies, waits for them, and re-layouts  27.7 us
    dot_general x1, matrix products, transform(): lax.dot_general(grouped, kron_table, (((3, 5), (0, 1)), ((), ())), precis...  24 us
    gather x1, local copies, waits for them, and re-layouts, local(): keep = (freqs[None, :] < jnp.take(lens, safe)[:, None]) & present[:, None]  23 us
    another operation x3, other arithmetic  18.5 us
  transfers between devices with their start and end apart: 6, of which 0 were waited for; matrix products, arithmetic and copies ran while one was open for 22% of the time, Pallas kernels for 0%

commit v1 on v0

v1 whole, which is shorter than its diff:
```python
import functools

import jax
import jax.numpy as jnp
from jax import lax
from jax.experimental import pallas as pl
from jax.experimental.pallas import tpu as pltpu
from jax.sharding import PartitionSpec as P

BY = 8
BZ = 16
COMP = 3
LANES = 128
MESH = pl.DeviceIdType.MESH


def dct_table(count):
    freqs = jnp.arange(count, dtype=jnp.float32)[:, None]
    points = jnp.arange(count, dtype=jnp.float32)[None, :]
    table = jnp.cos(jnp.pi * (points + 0.5) * freqs / count) * jnp.sqrt(2.0 / count)
    return jnp.where(freqs == 0.0, table * jnp.sqrt(0.5), table)


def split(value):
    high = value.astype(jnp.bfloat16)
    low = (value - high.astype(jnp.float32)).astype(jnp.bfloat16)
    return high, low


def dot(a, b):
    return jnp.dot(a, b, preferred_element_type=jnp.float32)


def iota(shape, dim):
    return lax.broadcasted_iota(jnp.int32, shape, dim)


def table_kernel(writers, cap, dest_ref, lens_ref, slots_ref, keep_ref):
    groups = dest_ref.shape[0]
    nblk = groups * LANES
    square = (LANES, LANES)
    upper = (iota(square, 0) < iota(square, 1)).astype(jnp.bfloat16)
    diagonal = iota(square, 0) == iota(square, 1)
    ones = jnp.ones(square, jnp.bfloat16)
    freqs = iota(square, 1).astype(jnp.float32)
    rows_w = iota((writers, LANES), 0)
    rows_s = iota((cap, LANES), 0).astype(jnp.float32)
    lane = iota((1, LANES), 1)
    count = jnp.zeros((writers, 1), jnp.float32)
    high = jnp.zeros((writers, cap), jnp.float32)
    low = jnp.zeros((writers, cap), jnp.float32)
    across = (((1,), (1,)), ((), ()))
    for group in range(groups):
        named = rows_w == dest_ref[pl.ds(group, 1), :]
        one = named.astype(jnp.float32)
        one_b = one.astype(jnp.bfloat16)
        before = dot(one_b, upper) + count
        rank = jnp.sum(one * before, axis=0, keepdims=True)
        at_slot = rows_s == rank
        number = lane + (group * LANES + 1)
        top = jnp.where(at_slot, (number // 64).astype(jnp.float32), 0.0).astype(jnp.bfloat16)
        rest = jnp.where(at_slot, (number % 64).astype(jnp.float32), 0.0).astype(jnp.bfloat16)
        high += lax.dot_general(one_b, top, across, preferred_element_type=jnp.float32)
        low += lax.dot_general(one_b, rest, across, preferred_element_type=jnp.float32)
        count += jnp.sum(one, axis=1, keepdims=True)
        lens = lens_ref[pl.ds(group, 1), :].astype(jnp.float32)
        spread = jnp.where(diagonal, jnp.broadcast_to(lens, square), 0.0).astype(jnp.bfloat16)
        keep_ref[pl.ds(group * LANES, LANES), :] = (freqs < dot(spread, ones)).astype(jnp.float32)
    code = (high * 64.0 + low).astype(jnp.int32)
    slots_ref[...] = jnp.where(code == 0, nblk, code - 1)


def exchange_kernel(
    sizes, velocity, slots, keep, table, received, total,
    field, y_out, y_in, z_out, z_in, turned, coeffs, rows, part, parts, plane_sum, plane_sums,
    in_sem, halo_send, halo_recv, row_send, row_recv, own_sem, part_send, part_recv, sum_send, sum_recv,
):
    n_gx, n_gy, n_wa, cells_x, cells_y, nblk, cap = sizes
    writers = n_gx * n_gy
    tiles_y = cells_y // 8
    gx, gy, wa = lax.axis_index("gx"), lax.axis_index("gy"), lax.axis_index("wa")
    me = gx * n_gy + gy

    def writer(w):
        return (w // n_gy, lax.rem(w, n_gy), wa)

    barrier = pltpu.get_barrier_semaphore()

    def greet(i, carry):
        pl.semaphore_signal(
            barrier, inc=1, device_id=writer(lax.rem(me + i, writers)), device_id_type=MESH
        )
        return carry

    lax.fori_loop(1, writers, greet, 0)
    for k in range(1, n_wa):
        pl.semaphore_signal(
            barrier, inc=1, device_id=(gx, gy, lax.rem(wa + k, n_wa)), device_id_type=MESH
        )

    loads = [
        pltpu.make_async_copy(
            velocity.at[c], field.at[c, pl.ds(cells_y, cells_x * cells_y)], in_sem.at[c]
        )
        for c in range(COMP)
    ]
    for load in loads:
        load.start()
    for load in loads:
        load.wait()

    lane = iota((8, LANES), 1)

    def pack_y(x, carry):
        for j, c in enumerate((0, 2)):
            first = field[c, pl.ds(cells_y + x * cells_y, 8), :]
            last = field[c, pl.ds(2 * cells_y - 8 + x * cells_y, 8), :]
            y_out[0, j, pl.ds(x, 1), :] = first[0:1]
            y_out[1, j, pl.ds(x, 1), :] = last[7:8]
        return carry

    lax.fori_loop(0, cells_x, pack_y, 0)

    packs = cells_x * tiles_y // LANES

    def pack_z(k, carry):
        out = []
        for j in range(2):
            for g in range(packs):
                tile = field[j, pl.ds(cells_y + (g * LANES + k) * 8, 8), :]
                low, high = carry[len(out)]
                low = jnp.where(lane == k, pltpu.roll(tile, k, 1), low)
                high = jnp.where(lane == k, pltpu.roll(tile, lax.rem(k + 1, LANES), 1), high)
                out.append((low, high))
        return tuple(out)

    zero = jnp.zeros((8, LANES), jnp.float32)
    packed = lax.fori_loop(0, LANES, pack_z, tuple((zero, zero) for _ in range(2 * packs)))
    for q, (low, high) in enumerate(packed):
        z_out[0, q] = low
        z_out[1, q] = high

    pl.semaphore_wait(barrier, writers - 1 + n_wa - 1)

    x_up = (lax.rem(gx + 1, n_gx), gy, wa)
    x_down = (lax.rem(gx + n_gx - 1, n_gx), gy, wa)
    y_up = (gx, lax.rem(gy + 1, n_gy), wa)
    y_down = (gx, lax.rem(gy + n_gy - 1, n_gy), wa)
    z_up = (gx, gy, lax.rem(wa + 1, n_wa))
    z_down = (gx, gy, lax.rem(wa + n_wa - 1, n_wa))
    faces = [
        (field.at[pl.ds(1, 2), pl.ds(cells_y, cells_y)],
         field.at[pl.ds(1, 2), pl.ds((cells_x + 1) * cells_y, cells_y)], x_down),
        (field.at[pl.ds(1, 2), pl.ds(cells_x * cells_y, cells_y)],
         field.at[pl.ds(1, 2), pl.ds(0, cells_y)], x_up),
        (y_out.at[0], y_in.at[0], y_down),
        (y_out.at[1], y_in.at[1], y_up),
        (z_out.at[0], z_in.at[0], z_down),
        (z_out.at[1], z_in.at[1], z_up),
    ]
    halos = [
        pltpu.make_async_remote_copy(
            src_ref=source, dst_ref=target, send_sem=halo_send.at[k], recv_sem=halo_recv.at[k],
            device_id=peer, device_id_type=MESH,
        )
        for k, (source, target, peer) in enumerate(faces)
    ]
    for halo in halos:
        halo.start()
    for halo in halos:
        halo.wait()

    row = iota((cells_y, LANES), 0)
    column = iota((cells_y, LANES), 1)
    group = column // BZ
    lower = []
    for step in (4, 2, 1):
        row_bit = (row // step) % 2
        group_bit = (group // step) % 2
        lower.append((step, (row_bit == 0) & (group_bit == 1), (row_bit == 1) & (group_bit == 0)))

    def turn(plane):
        for step, up, down in lower:
            ahead = pltpu.roll(pltpu.roll(plane, BZ * step, 1), cells_y - step, 0)
            behind = pltpu.roll(pltpu.roll(plane, LANES - BZ * step, 1), step, 0)
            plane = jnp.where(up, ahead, jnp.where(down, behind, plane))
        return plane

    def along_x(c, x):
        after = field[c, pl.ds((x + 2) * cells_y, cells_y), :]
        return after - field[c, pl.ds(x * cells_y, cells_y), :]

    def along_y(plane, j, x):
        after = jnp.where(row == cells_y - 1, y_in[0, j, pl.ds(x, 1), :], pltpu.roll(plane, cells_y - 1, 0))
        before = jnp.where(row == 0, y_in[1, j, pl.ds(x, 1), :], pltpu.roll(plane, 1, 0))
        return after - before

    def along_z(plane, j, x):
        per = LANES // tiles_y
        q = j * packs + x // per
        base = lax.rem(x, per) * tiles_y
        nexts, lasts = z_in[0, q], z_in[1, q]
        after = jnp.concatenate(
            [pltpu.roll(nexts, LANES - 1 - base - t, 1) for t in range(tiles_y)], axis=0
        )
        before = jnp.concatenate(
            [pltpu.roll(lasts, lax.rem(LANES - base - t, LANES), 1) for t in range(tiles_y)], axis=0
        )
        after = jnp.where(column == LANES - 1, after, pltpu.roll(plane, LANES - 1, 1))
        before = jnp.where(column == 0, before, pltpu.roll(plane, 1, 1))
        return after - before

    def curl(x, square):
        here = pl.ds((x + 1) * cells_y, cells_y)
        u, v, w = field[0, here, :], field[1, here, :], field[2, here, :]
        first = (along_y(w, 1, x) - along_z(v, 1, x)) * 0.5
        second = (along_z(u, 0, x) - along_x(2, x)) * 0.5
        third = (along_x(1, x) - along_y(u, 0, x)) * 0.5
        for c, plane in enumerate((first, second, third)):
            turned[c, pl.ds(x * cells_y, cells_y), :] = turn(plane)
            square += plane * plane
        return square

    square = lax.fori_loop(0, cells_x, curl, jnp.zeros((cells_y, LANES), jnp.float32))
    part[...] = jnp.sum(square.reshape(tiles_y, 8, LANES), axis=0)
    parts[pl.ds(me, 1)] = part[...][None]

    def part_copy(i, peer, slot):
        return pltpu.make_async_remote_copy(
            src_ref=part, dst_ref=parts.at[slot], send_sem=part_send.at[i],
            recv_sem=part_recv.at[i], device_id=writer(peer), device_id_type=MESH,
        )

    def part_start(i, carry):
        part_copy(i, lax.rem(me + i, writers), me).start()
        return carry

    lax.fori_loop(1, writers, part_start, 0)

    coeffs[pl.ds(nblk, 8), :] = zero
    chunk = 2 * LANES

    def row_copy(c, i, peer, slot):
        return pltpu.make_async_remote_copy(
            src_ref=rows.at[c, peer], dst_ref=received.at[c, slot], send_sem=row_send.at[c, i],
            recv_sem=row_recv.at[c, i], device_id=writer(peer), device_id_type=MESH,
        )

    def own_copy(c):
        return pltpu.make_async_copy(rows.at[c, me], received.at[c, me], own_sem.at[c])

    for c in range(COMP):

        def transform(k, carry):
            at = pl.ds(k * chunk, chunk)
            high, low = split(turned[c, at, :])
            value = dot(high, table[0]) + (dot(low, table[0]) + dot(high, table[1]))
            coeffs[at, :] = value * keep[at, :]
            return carry

        lax.fori_loop(0, nblk // chunk, transform, 0)

        def gather(i):
            w = lax.rem(me + i, writers)
            for s in range(cap):
                rows[c, w, pl.ds(s, 1), :] = coeffs[pl.ds(slots[w, s], 1), :]

        def send(i):
            row_copy(c, i, lax.rem(me + i, writers), me).start()

        gather(1)

        def step(i, carry):
            gather(i)
            send(i - 1)
            return carry

        lax.fori_loop(2, writers, step, 0)
        gather(0)
        send(writers - 1)
        own_copy(c).start()

        if c == 0:

            def part_wait(i, carry):
                part_copy(i, lax.rem(me + i, writers), lax.rem(me + writers - i, writers)).wait()
                return carry

            lax.fori_loop(1, writers, part_wait, 0)
            plane_sum[...] = jnp.sum(parts[...], axis=0)
            plane_sums[pl.ds(wa, 1)] = plane_sum[...][None]
            sums = [
                pltpu.make_async_remote_copy(
                    src_ref=plane_sum, dst_ref=plane_sums.at[wa], send_sem=sum_send.at[k],
                    recv_sem=sum_recv.at[k], device_id=(gx, gy, lax.rem(wa + k, n_wa)),
                    device_id_type=MESH,
                )
                for k in range(1, n_wa)
            ]
            for copy in sums:
                copy.start()

    for k in range(1, n_wa):
        pltpu.make_async_remote_copy(
            src_ref=plane_sum, dst_ref=plane_sums.at[lax.rem(wa + n_wa - k, n_wa)],
            send_sem=sum_send.at[k], recv_sem=sum_recv.at[k],
            device_id=(gx, gy, lax.rem(wa + k, n_wa)), device_id_type=MESH,
        ).wait()
    total[...] = jnp.sum(plane_sums[...], axis=0)

    for c in range(COMP):
        own_copy(c).wait()

        def row_wait(i, carry):
            row_copy(c, i, lax.rem(me + i, writers), lax.rem(me + writers - i, writers)).wait()
            return carry

        lax.fori_loop(1, writers, row_wait, 0)


def local(n_gx, n_gy, n_wa, velocity, lengths, destinations):
    comps, cells_x, cells_y, cells_z = velocity.shape
    nblk = lengths.size
    writers = n_gx * n_gy
    cap = max(2, 2 * nblk // writers)
    whole = pl.BlockSpec(memory_space=pltpu.VMEM)
    slots, keep = pl.pallas_call(
        functools.partial(table_kernel, writers, cap),
        out_shape=(
            jax.ShapeDtypeStruct((writers, cap), jnp.int32),
            jax.ShapeDtypeStruct((nblk, LANES), jnp.float32),
        ),
        in_specs=[whole, whole],
        out_specs=(whole, whole),
    )(destinations.reshape(nblk // LANES, LANES), lengths.reshape(nblk // LANES, LANES))
    exact = jnp.kron(dct_table(BY), dct_table(BZ)).T
    high = lax.reduce_precision(exact, 8, 7)
    table = jnp.stack([high, exact - high]).astype(jnp.bfloat16)
    sizes = (n_gx, n_gy, n_wa, cells_x, cells_y, nblk, cap)
    f32 = jnp.float32
    packs = cells_x * cells_y // 8 // LANES
    dma = pltpu.SemaphoreType.DMA
    received, total = pl.pallas_call(
        functools.partial(exchange_kernel, sizes),
        out_shape=(
            jax.ShapeDtypeStruct((comps, writers, cap, LANES), f32),
            jax.ShapeDtypeStruct((8, LANES), f32),
        ),
        in_specs=[
            pl.BlockSpec(memory_space=pl.ANY),
            pl.BlockSpec(memory_space=pltpu.SMEM),
            whole,
            whole,
        ],
        out_specs=(pl.BlockSpec(memory_space=pl.ANY), whole),
        scratch_shapes=[
            pltpu.VMEM((comps, (cells_x + 2) * cells_y, LANES), f32),
            pltpu.VMEM((2, 2, cells_x, LANES), f32),
            pltpu.VMEM((2, 2, cells_x, LANES), f32),
            pltpu.VMEM((2, 2 * packs, 8, LANES), f32),
            pltpu.VMEM((2, 2 * packs, 8, LANES), f32),
            pltpu.VMEM((comps, nblk, LANES), f32),
            pltpu.VMEM((nblk + 8, LANES), f32),
            pltpu.VMEM((comps, writers, cap, LANES), f32),
            pltpu.VMEM((8, LANES), f32),
            pltpu.VMEM((writers, 8, LANES), f32),
            pltpu.VMEM((8, LANES), f32),
            pltpu.VMEM((n_wa, 8, LANES), f32),
            dma((comps,)),
            dma((6,)),
            dma((6,)),
            dma((comps, writers)),
            dma((comps, writers)),
            dma((comps,)),
            dma((writers,)),
            dma((writers,)),
            dma((n_wa,)),
            dma((n_wa,)),
        ],
        compiler_params=pltpu.CompilerParams(
            collective_id=0, has_side_effects=True, vmem_limit_bytes=32 * 2**20
        ),
    )(velocity.reshape(comps, cells_x * cells_y, cells_z), slots, keep, table)
    every = velocity.size * n_gx * n_gy * n_wa
    rms = jnp.sqrt(jnp.sum(total) / every + 1e-06)
    return (received * (1.0 / rms)).reshape(1, 1, comps, writers, cap, LANES)


def solution(mesh):
    n_gx, n_gy, n_wa = mesh.shape["gx"], mesh.shape["gy"], mesh.shape["wa"]
    return jax.shard_map(
        functools.partial(local, n_gx, n_gy, n_wa),
        mesh=mesh,
        in_specs=(
            P(None, "gx", "gy", "wa"),
            P("gx", "gy", "wa", None),
            P("gx", "gy", "wa", None, None),
        ),
        out_specs=P(("gx", "gy"), "wa", None, None, None, None),
        check_vma=False,
    )
```

time: 448 us -> 206 us (0.46)
  Pallas kernels: 0 us -> 190 us
  blocking collectives: 190 us -> 0 us
  local copies, waits for them, and re-layouts: 149 us -> 6.76 us
  other arithmetic: 71.2 us -> 7.86 us
  matrix products: 24 us -> 0 us
  starting transfers between devices: 10.9 us -> 0 us
    pallas_call x0 -> x2, Pallas kernels: none -> 190 us  [the longest x1 185 us: local(): pl.pallas_call(functools.partial(exchange_kernel, sizes), out_shape=(jax....]
    all_to_all x1 -> x0, blocking collectives: 151 us -> none  [local(): lax.all_to_all(outgoing, GX_GY, split_axis=1, concat_axis=1, tiled=True)]
    gather x2 -> x0, local copies, waits for them, and re-layouts: 55.5 us -> none  [the longest x1 32.5 us: local(): picked = jnp.take(coeffs, safe, axis=1)]
    psum x4 -> x0, blocking collectives: 38.8 us -> none  [over_axes(): array = lax.psum(array, axis)]
    dot_general x2 -> x0, local copies, waits for them, and re-layouts: 33 us -> none  [transform(): lax.dot_general(grouped, kron_table, (((3, 5), (0, 1)), ((), ())), precis...]
    sub x2 -> x0, other arithmetic: 28.8 us -> none  [the longest x1 18.5 us: curl_field(): first = along_y(2) - along_z(1)]
    dot_general x1 -> x0, matrix products: 24 us -> none  [transform(): lax.dot_general(grouped, kron_table, (((3, 5), (0, 1)), ((), ())), precis...]
    unnamed x25 -> x8, local copies, waits for them, and re-layouts: 27.7 us -> 6.57 us
  transfers between devices with their start and end apart: 6 -> 0, of which waited for: 0 -> 0; matrix products, arithmetic and copies ran while one was open for 22% -> 0% of each run, Pallas kernels for 0% -> 0%
where the time goes in v1:
time: 206 us; the launch traced here: 205 us
  Pallas kernels  190 us (92%)
  other arithmetic  7.86 us (4%)
  local copies, waits for them, and re-layouts  6.76 us (3%)
    pallas_call x1, Pallas kernels, local(): pl.pallas_call(functools.partial(exchange_kernel, sizes), out_shape=(jax....  185 us
    reshape x1, other arithmetic, local(): return (received * (1.0 / rms)).reshape(1, 1, comps, writers, cap, LANES)  6.86 us
    unnamed x8, local copies, waits for them, and re-layouts  6.57 us
    pallas_call x1, Pallas kernels, local(): pl.pallas_call(functools.partial(table_kernel, writers, cap), out_shape=(...  4.54 us

profile of v1, /device:TPU:1, one launch (start us, length us, event | category | flops | bytes accessed | tf_op | source)
XLA Modules:
  0.0 205.1 jit_solution(12588110627655380326)
XLA Ops:
  0.1 0.1 multiply_select_fusion.1
  0.2 0.1 multiply_select_fusion
  0.3 0.1 broadcast_multiply_fusion
  0.4 0.2 mul.139
  0.6 4.5 %shard_map.37 = (s32[64,64]{1,0:T(8,128)}, f32[2048,128]{1,0:T(8,128)}) custom-call(s32[16,128]{1,0:T(8,128)} %bitcast.21, s32[16,128]{1,0:T(8,128)} %bitcast.22), custom_call_target="tpu_custom_call" | custom-call | tf_op jit(solution)/shard_map/pallas_call | solution.py:327
  5.2 0.0 copy-start.1
  5.2 1.9 copy-done.1
  7.1 0.0 copy-start.2
  7.1 1.2 copy-done.2
  8.3 0.0 copy-start.3
  8.3 0.8 copy-done.3
  9.1 185.2 %shard_map.38 = (f32[3,64,64,128]{3,2,1,0:T(8,128)S(1)}, f32[8,128]{1,0:T(8,128)S(1)}) custom-call(f32[3,2048,128]{2,1,0:T(8,128)S(1)} %bitcast.20, s32[64,64]{1,0:T(8,128)S(1)} %copy-done.3, f32[2048,128]{1,0:T(8,128)S(1)} %copy-done.2, bf16[2,128,128]{2,1,0:T(8,128)(2,1)S(1)} %pad_maximum_fusion.table), custom_call_target="tpu_custom_call" | custom-call | tf_op jit(solution)/shard_map/pallas_call | solution.py:343
  194.2 0.0 copy-start
  194.2 2.7 %copy-done = f32[3,64,64,128]{3,2,1,0:T(8,128)} copy-done((f32[3,64,64,128]{3,2,1,0:T(8,128)}, f32[3,64,64,128]{3,2,1,0:T(8,128)S(1)}, u32[]{:S(2)}) %copy-start) | copy-done | bytes 6291480
  196.9 0.6 reduce_sum.9
  198.2 6.9 %multiply_bitcast_fusion = f32[1,1,3,64,64,128]{5,4,3,2,1,0:T(8,128)} fusion(f32[3,64,64,128]{3,2,1,0:T(8,128)} %copy-done, f32[]{:T(128)S(6)} %sqrt.3), kind=kLoop, calls=%fused_computation | loop fusion | flops 1572864 | bytes 12582916 | tf_op jit(solution)/shard_map/reshape | solution.py:386
  (6 shorter events, 0.1 us)
Async XLA Ops:
  5.2 1.9 copy-start.1
  7.1 1.2 copy-start.2
  8.3 0.8 copy-start.3
  194.2 2.7 %copy-start = (f32[3,64,64,128]{3,2,1,0:T(8,128)}, f32[3,64,64,128]{3,2,1,0:T(8,128)S(1)}, u32[]{:S(2)}) copy-start(f32[3,64,64,128]{3,2,1,0:T(8,128)S(1)} %get-tuple-element.11) | copy-start | bytes 18874372

commit v2 on v1

v2 whole, which is shorter than its diff:
```python
import functools

import jax
import jax.numpy as jnp
from jax import lax
from jax.experimental import pallas as pl
from jax.experimental.pallas import tpu as pltpu
from jax.sharding import PartitionSpec as P

BY = 8
BZ = 16
COMP = 3
LANES = 128
MESH = pl.DeviceIdType.MESH


def dct_table(count):
    freqs = jnp.arange(count, dtype=jnp.float32)[:, None]
    points = jnp.arange(count, dtype=jnp.float32)[None, :]
    table = jnp.cos(jnp.pi * (points + 0.5) * freqs / count) * jnp.sqrt(2.0 / count)
    return jnp.where(freqs == 0.0, table * jnp.sqrt(0.5), table)


def split(value):
    high = value.astype(jnp.bfloat16)
    low = (value - high.astype(jnp.float32)).astype(jnp.bfloat16)
    return high, low


def dot(a, b):
    return jnp.dot(a, b, preferred_element_type=jnp.float32)


def iota(shape, dim):
    return lax.broadcasted_iota(jnp.int32, shape, dim)


def turned_row(block):
    return block // 64 * 64 + block % 8 * 8 + block // 8 % 8


def make_table(writers, cap, dest_ref, lens_ref, slots_ref, keep_ref):
    groups = dest_ref.shape[0]
    nblk = groups * LANES
    square = (LANES, LANES)
    upper = (iota(square, 0) < iota(square, 1)).astype(jnp.bfloat16)
    diagonal = iota(square, 0) == turned_row(iota(square, 1))
    ones = jnp.ones(square, jnp.bfloat16)
    freqs = iota(square, 1).astype(jnp.float32)
    rows_w = iota((writers, LANES), 0)
    rows_s = iota((cap, LANES), 0).astype(jnp.float32)
    lane = iota((1, LANES), 1)
    count = jnp.zeros((writers, 1), jnp.float32)
    high = jnp.zeros((writers, cap), jnp.float32)
    low = jnp.zeros((writers, cap), jnp.float32)
    across = (((1,), (1,)), ((), ()))
    for group in range(groups):
        named = rows_w == dest_ref[pl.ds(group, 1), :]
        one = named.astype(jnp.float32)
        one_b = one.astype(jnp.bfloat16)
        before = dot(one_b, upper) + count
        rank = jnp.sum(one * before, axis=0, keepdims=True)
        at_slot = rows_s == rank
        number = turned_row(lane) + (group * LANES + 1)
        top = jnp.where(at_slot, (number // 64).astype(jnp.float32), 0.0).astype(jnp.bfloat16)
        rest = jnp.where(at_slot, (number % 64).astype(jnp.float32), 0.0).astype(jnp.bfloat16)
        high += lax.dot_general(one_b, top, across, preferred_element_type=jnp.float32)
        low += lax.dot_general(one_b, rest, across, preferred_element_type=jnp.float32)
        count += jnp.sum(one, axis=1, keepdims=True)
        lens = lens_ref[pl.ds(group, 1), :].astype(jnp.float32)
        spread = jnp.where(diagonal, jnp.broadcast_to(lens, square), 0.0).astype(jnp.bfloat16)
        keep_ref[pl.ds(group * LANES, LANES), :] = (freqs < dot(spread, ones)).astype(jnp.float32)
    code = (high * 64.0 + low).astype(jnp.int32)
    slots_ref[...] = jnp.clip(jnp.where(code == 0, nblk, code - 1), 0, nblk)


def exchange_kernel(
    sizes, field, dest, lens, table, result,
    x_in, y_out, y_in, z_out, z_in, turned, coeffs, rows, received, keep, slots_v, slots,
    part, parts, plane_sum, plane_sums,
    halo_send, halo_recv, row_send, row_recv, own_sem, out_sem, slot_sem,
    part_send, part_recv, sum_send, sum_recv,
):
    n_gx, n_gy, n_wa, cells_x, cells_y, nblk, cap = sizes
    writers = n_gx * n_gy
    tiles_y = cells_y // 8
    gx, gy, wa = lax.axis_index("gx"), lax.axis_index("gy"), lax.axis_index("wa")
    me = gx * n_gy + gy

    def writer(w):
        return (w // n_gy, lax.rem(w, n_gy), wa)

    barrier = pltpu.get_barrier_semaphore()

    def greet(i, carry):
        pl.semaphore_signal(
            barrier, inc=1, device_id=writer(lax.rem(me + i, writers)), device_id_type=MESH
        )
        return carry

    lax.fori_loop(1, writers, greet, 0)
    for k in range(1, n_wa):
        pl.semaphore_signal(
            barrier, inc=1, device_id=(gx, gy, lax.rem(wa + k, n_wa)), device_id_type=MESH
        )

    lane = iota((8, LANES), 1)
    sub = iota((8, LANES), 0)
    zero = jnp.zeros((8, LANES), jnp.float32)
    packs = cells_x * 8 // LANES
    per = cells_x // packs

    def tile(c, x, y):
        return field[c, pl.ds(x * cells_y + y, tiles_y, stride=8), :]

    def pack_y(c, j):
        def pack(x, carry):
            y_out[0, j, pl.ds(x, 1), :] = field[c, pl.ds(x * cells_y, 1), :]
            y_out[1, j, pl.ds(x, 1), :] = field[c, pl.ds((x + 1) * cells_y - 1, 1), :]
            return carry

        lax.fori_loop(0, cells_x, pack, 0)

    def pack_z(c, j):
        for g in range(packs):

            def pack(step, carry):
                low, high = carry
                for x, y in [(x, y) for x in range(2) for y in range(8)]:
                    k = (step * 2 + x) * 8 + y
                    here = tile(c, g * per + step * 2 + x, y)
                    low = jnp.where(lane == k, pltpu.roll(here, k, 1), low)
                    high = jnp.where(lane == k, pltpu.roll(here, lax.rem(k + 1, LANES), 1), high)
                return low, high

            low, high = lax.fori_loop(0, per // 2, pack, (zero, zero))
            z_out[0, j, g] = low
            z_out[1, j, g] = high

    x_up = (lax.rem(gx + 1, n_gx), gy, wa)
    x_down = (lax.rem(gx + n_gx - 1, n_gx), gy, wa)
    y_up = (gx, lax.rem(gy + 1, n_gy), wa)
    y_down = (gx, lax.rem(gy + n_gy - 1, n_gy), wa)
    z_up = (gx, gy, lax.rem(wa + 1, n_wa))
    z_down = (gx, gy, lax.rem(wa + n_wa - 1, n_wa))
    faces = [
        (z_out.at[0, 1], z_in.at[0, 1], z_down),
        (z_out.at[1, 1], z_in.at[1, 1], z_up),
        (y_out.at[0, 1], y_in.at[0, 1], y_down),
        (y_out.at[1, 1], y_in.at[1, 1], y_up),
        (z_out.at[0, 0], z_in.at[0, 0], z_down),
        (z_out.at[1, 0], z_in.at[1, 0], z_up),
        (y_out.at[0, 0], y_in.at[0, 0], y_down),
        (y_out.at[1, 0], y_in.at[1, 0], y_up),
        (field.at[pl.ds(1, 2), pl.ds(0, cells_y)], x_in.at[0], x_down),
        (field.at[pl.ds(1, 2), pl.ds((cells_x - 1) * cells_y, cells_y)], x_in.at[1], x_up),
    ]
    halos = [
        pltpu.make_async_remote_copy(
            src_ref=source, dst_ref=target, send_sem=halo_send.at[k], recv_sem=halo_recv.at[k],
            device_id=peer, device_id_type=MESH,
        )
        for k, (source, target, peer) in enumerate(faces)
    ]

    pack_z(1, 1)
    pack_y(2, 1)
    pack_z(0, 0)
    pack_y(0, 0)
    make_table(writers, cap, dest, lens, slots_v, keep)
    slot_copy = pltpu.make_async_copy(slots_v, slots, slot_sem)
    slot_copy.start()
    pl.semaphore_wait(barrier, writers - 1 + n_wa - 1)
    for halo in halos:
        halo.start()
    coeffs[pl.ds(nblk, 8), :] = zero

    group = lane // BZ

    def turn(tiles):
        for step in (4, 2, 1):
            bit = (group // step) % 2 == 1
            out = list(tiles)
            for a in range(8):
                if a & step == 0:
                    b = a | step
                    out[a] = jnp.where(bit, pltpu.roll(tiles[b], BZ * step, 1), tiles[a])
                    out[b] = jnp.where(bit, tiles[b], pltpu.roll(tiles[a], LANES - BZ * step, 1))
            tiles = out
        return tiles

    def along_x(c, x, edge):
        def near(at, d):
            if edge == d:
                return [x_in[d, c - 1, pl.ds(y, tiles_y, stride=8), :] for y in range(8)]
            return [tile(c, at, y) for y in range(8)]

        return [a - b for a, b in zip(near(x + 1, 0), near(x - 1, 1))]

    def along_y(c, j, x):
        here = [tile(c, x, y) for y in range(8)]
        after = jnp.where(sub == tiles_y - 1, y_in[0, j, pl.ds(x, 1), :], pltpu.roll(here[0], tiles_y - 1, 0))
        before = jnp.where(sub == 0, y_in[1, j, pl.ds(x, 1), :], pltpu.roll(here[7], 1, 0))
        return [a - b for a, b in zip(here[1:] + [after], [before] + here[:-1])]

    def along_z(c, j, x):
        nexts, lasts = z_in[0, j, x // per], z_in[1, j, x // per]
        out = []
        for y in range(8):
            k = lax.rem(x, per) * 8 + y
            here = tile(c, x, y)
            after = jnp.where(
                lane == LANES - 1, pltpu.roll(nexts, LANES - 1 - k, 1), pltpu.roll(here, LANES - 1, 1)
            )
            before = jnp.where(
                lane == 0, pltpu.roll(lasts, lax.rem(LANES - k, LANES), 1), pltpu.roll(here, 1, 1)
            )
            out.append(after - before)
        return out

    def curl(c, square):
        def at(x, square, edge=None):
            if c == 0:
                pairs = zip(along_y(2, 1, x), along_z(1, 1, x))
            elif c == 1:
                pairs = zip(along_z(0, 0, x), along_x(2, x, edge))
            else:
                pairs = zip(along_x(1, x, edge), along_y(0, 0, x))
            tiles = [(a - b) * 0.5 for a, b in pairs]
            for t in tiles:
                square += t * t
            for z, t in enumerate(turn(tiles)):
                turned[c, pl.ds(x * cells_y + z * tiles_y, tiles_y), :] = t
            return square

        if c == 0:
            return lax.fori_loop(0, cells_x // 2, lambda i, q: at(2 * i + 1, at(2 * i, q)), square)
        square = at(0, square, 1)
        square = lax.fori_loop(1, cells_x - 1, at, square)
        return at(cells_x - 1, square, 0)

    chunk = 2 * LANES

    def row_copy(c, i, slot):
        peer = lax.rem(me + i, writers)
        return pltpu.make_async_remote_copy(
            src_ref=rows.at[c, peer], dst_ref=received.at[c, slot], send_sem=row_send.at[c, i],
            recv_sem=row_recv.at[c, i], device_id=writer(peer), device_id_type=MESH,
        )

    def own_copy(c):
        return pltpu.make_async_copy(rows.at[c, me], received.at[c, me], own_sem.at[c])

    def deliver(c):
        def transform(k, carry):
            at = pl.ds(k * chunk, chunk)
            high, low = split(turned[c, at, :])
            value = dot(high, table[0]) + (dot(low, table[0]) + dot(high, table[1]))
            coeffs[at, :] = value * keep[at, :]
            return carry

        lax.fori_loop(0, nblk // chunk, transform, 0)

        def gather(i):
            w = lax.rem(me + i, writers)
            for s in range(cap):
                rows[c, w, pl.ds(s, 1), :] = coeffs[pl.ds(slots[w, s], 1), :]

        gather(1)

        def step(i, carry):
            gather(i)
            row_copy(c, i - 1, me).start()
            return carry

        lax.fori_loop(2, writers, step, 0)
        gather(0)
        row_copy(c, writers - 1, me).start()
        own_copy(c).start()

    def part_copy(i, slot):
        return pltpu.make_async_remote_copy(
            src_ref=part, dst_ref=parts.at[slot], send_sem=part_send.at[i],
            recv_sem=part_recv.at[i], device_id=writer(lax.rem(me + i, writers)),
            device_id_type=MESH,
        )

    def sum_copy(k, slot):
        return pltpu.make_async_remote_copy(
            src_ref=plane_sum, dst_ref=plane_sums.at[slot], send_sem=sum_send.at[k],
            recv_sem=sum_recv.at[k], device_id=(gx, gy, lax.rem(wa + k, n_wa)),
            device_id_type=MESH,
        )

    for halo in halos[:4]:
        halo.wait()
    square = curl(0, zero)
    slot_copy.wait()
    deliver(0)
    for halo in halos[4:]:
        halo.wait()
    square = curl(2, curl(1, square))
    part[...] = square
    parts[pl.ds(me, 1)] = part[...][None]

    def part_start(i, carry):
        part_copy(i, me).start()
        return carry

    lax.fori_loop(1, writers, part_start, 0)
    deliver(1)
    deliver(2)

    def part_wait(i, carry):
        part_copy(i, lax.rem(me + writers - i, writers)).wait()
        return carry

    lax.fori_loop(1, writers, part_wait, 0)
    plane_sum[...] = jnp.sum(parts[...], axis=0)
    plane_sums[pl.ds(wa, 1)] = plane_sum[...][None]
    for k in range(1, n_wa):
        sum_copy(k, wa).start()
    for k in range(1, n_wa):
        sum_copy(k, lax.rem(wa + n_wa - k, n_wa)).wait()
    total = jnp.sum(plane_sums[...], axis=0)
    total = jnp.sum(jnp.sum(total, axis=0, keepdims=True), axis=1, keepdims=True)
    every = COMP * cells_x * cells_y * LANES * writers * n_wa
    scale = 1.0 / jnp.sqrt(total / every + 1e-06)
    scale = jnp.broadcast_to(jnp.broadcast_to(scale, (1, LANES)), (cap, LANES))

    for c in range(COMP):
        own_copy(c).wait()

        def row_wait(i, carry):
            row_copy(c, i, lax.rem(me + writers - i, writers)).wait()
            return carry

        lax.fori_loop(1, writers, row_wait, 0)

        def rescale(s, carry):
            received[c, s] = received[c, s] * scale
            return carry

        lax.fori_loop(0, writers, rescale, 0)
        pltpu.make_async_copy(received.at[c], result.at[c], out_sem.at[c]).start()
    for c in range(COMP):
        pltpu.make_async_copy(received.at[c], result.at[c], out_sem.at[c]).wait()


def local(n_gx, n_gy, n_wa, velocity, lengths, destinations):
    comps, cells_x, cells_y, cells_z = velocity.shape
    nblk = lengths.size
    writers = n_gx * n_gy
    cap = max(2, 2 * nblk // writers)
    whole = pl.BlockSpec(memory_space=pltpu.VMEM)
    exact = jnp.kron(dct_table(BY), dct_table(BZ)).T
    high = lax.reduce_precision(exact, 8, 7)
    table = jnp.stack([high, exact - high]).astype(jnp.bfloat16)
    sizes = (n_gx, n_gy, n_wa, cells_x, cells_y, nblk, cap)
    f32 = jnp.float32
    packs = cells_x * cells_y // 8 // LANES
    dma = pltpu.SemaphoreType.DMA
    result = pl.pallas_call(
        functools.partial(exchange_kernel, sizes),
        out_shape=jax.ShapeDtypeStruct((comps, writers, cap, LANES), f32),
        in_specs=[whole, whole, whole, whole],
        out_specs=pl.BlockSpec(memory_space=pl.ANY),
        scratch_shapes=[
            pltpu.VMEM((2, 2, cells_y, LANES), f32),
            pltpu.VMEM((2, 2, cells_x, LANES), f32),
            pltpu.VMEM((2, 2, cells_x, LANES), f32),
            pltpu.VMEM((2, 2, packs, 8, LANES), f32),
            pltpu.VMEM((2, 2, packs, 8, LANES), f32),
            pltpu.VMEM((comps, nblk, LANES), f32),
            pltpu.VMEM((nblk + 8, LANES), f32),
            pltpu.VMEM((comps, writers, cap, LANES), f32),
            pltpu.VMEM((comps, writers, cap, LANES), f32),
            pltpu.VMEM((nblk, LANES), f32),
            pltpu.VMEM((writers, cap), jnp.int32),
            pltpu.SMEM((writers, cap), jnp.int32),
            pltpu.VMEM((8, LANES), f32),
            pltpu.VMEM((writers, 8, LANES), f32),
            pltpu.VMEM((8, LANES), f32),
            pltpu.VMEM((n_wa, 8, LANES), f32),
            dma((10,)),
            dma((10,)),
            dma((comps, writers)),
            dma((comps, writers)),
            dma((comps,)),
            dma((comps,)),
            dma,
            dma((writers,)),
            dma((writers,)),
            dma((n_wa,)),
            dma((n_wa,)),
        ],
        compiler_params=pltpu.CompilerParams(
            collective_id=0, has_side_effects=True, vmem_limit_bytes=40 * 2**20
        ),
    )(
        velocity.reshape(comps, cells_x * cells_y, cells_z),
        destinations.reshape(nblk // LANES, LANES),
        lengths.reshape(nblk // LANES, LANES),
        table,
    )
    return result.reshape(1, 1, comps, writers, cap, LANES)


def solution(mesh):
    n_gx, n_gy, n_wa = mesh.shape["gx"], mesh.shape["gy"], mesh.shape["wa"]
    return jax.shard_map(
        functools.partial(local, n_gx, n_gy, n_wa),
        mesh=mesh,
        in_specs=(
            P(None, "gx", "gy", "wa"),
            P("gx", "gy", "wa", None),
            P("gx", "gy", "wa", None, None),
        ),
        out_specs=P(("gx", "gy"), "wa", None, None, None, None),
        check_vma=False,
    )
```

time: 206 us -> 180 us (0.87)
  Pallas kernels: 190 us -> 172 us
  other arithmetic: 7.86 us -> 0.4 us
    pallas_call x2 -> x1, Pallas kernels: 190 us -> 172 us  [local(): pl.pallas_call(functools.partial(exchange_kernel, sizes), out_shape=jax.S...]
    reshape x1 -> x0, other arithmetic: 6.86 us -> none  [local(): return (received * (1.0 / rms)).reshape(1, 1, comps, writers, cap, LANES)]
    unnamed x8 -> x7, local copies, waits for them, and re-layouts: 6.57 us -> 5.98 us
where the time goes in v2:
time: 180 us; the launch traced here: 178 us
  Pallas kernels  172 us (96%)
  local copies, waits for them, and re-layouts  6.17 us (3%)
    pallas_call x1, Pallas kernels, local(): pl.pallas_call(functools.partial(exchange_kernel, sizes), out_shape=jax.S...  172 us
    unnamed x7, local copies, waits for them, and re-layouts  5.98 us

profile of v2, /device:TPU:1, one launch (start us, length us, event | category | flops | bytes accessed | tf_op | source)
XLA Modules:
  0.0 178.3 jit_solution(16885940462344430543)
XLA Ops:
  0.1 0.1 multiply_select_fusion.1
  0.2 0.1 multiply_select_fusion
  0.3 0.1 broadcast_multiply_fusion
  0.4 0.2 mul.133
  0.6 0.0 copy-start
  0.6 1.9 %copy-done = f32[3,32,64,128]{3,2,1,0:T(8,128)S(1)} copy-done((f32[3,32,64,128]{3,2,1,0:T(8,128)S(1)}, f32[3,32,64,128]{3,2,1,0:T(8,128)}, u32[]{:S(2)}) %copy-start) | copy-done | bytes 3145752
  2.5 0.0 copy-start.1
  2.5 0.7 copy-done.1
  3.2 0.0 copy-start.2
  3.2 0.7 copy-done.2
  3.9 171.7 %shard_map.37 = f32[3,64,64,128]{3,2,1,0:T(8,128)S(1)} custom-call(f32[3,2048,128]{2,1,0:T(8,128)S(1)} %bitcast.20, s32[16,128]{1,0:T(8,128)S(1)} %bitcast.21, s32[16,128]{1,0:T(8,128)S(1)} %bitcast.22, bf16[2,128,128]{2,1,0:T(8,128)(2,1)S(1)} %pad_maximum_fusion.table), custom_call_target="tpu_custom_call" | custom-call | tf_op jit(solution)/shard_map/pallas_call | solution.py:363
  175.6 2.7 %copy.5 = f32[1,1,3,64,64,128]{5,4,3,2,1,0:T(8,128)} copy(f32[1,1,3,64,64,128]{5,4,3,2,1,0:T(8,128)S(1)} %bitcast.19) | data formatting | bytes 12582912
  (6 shorter events, 0.1 us)
Async XLA Ops:
  0.6 1.9 %copy-start = (f32[3,32,64,128]{3,2,1,0:T(8,128)S(1)}, f32[3,32,64,128]{3,2,1,0:T(8,128)}, u32[]{:S(2)}) copy-start(f32[3,32,64,128]{3,2,1,0:T(8,128)} %param.3) | copy-start | bytes 9437188
  2.5 0.7 copy-start.1
  3.2 0.7 copy-start.2

commit v3 on v2

--- a/solution.py
+++ b/solution.py
@@ -74,6 +74,71 @@
     slots_ref[...] = jnp.clip(jnp.where(code == 0, nblk, code - 1), 0, nblk)
 
 
+def make_packing(n_gx, n_gy, most, dest_ref, lens_ref, first_ref, second_ref, codes_ref, keep_ref):
+    writers = n_gx * n_gy
+    groups = dest_ref.shape[0]
+    nblk = groups * LANES
+    square = (LANES, LANES)
+    upper = (iota(square, 0) < iota(square, 1)).astype(jnp.bfloat16)
+    diagonal = iota(square, 0) == turned_row(iota(square, 1))
+    ones = jnp.ones(square, jnp.bfloat16)
+    freqs = iota(square, 1).astype(jnp.float32)
+    rows_w = iota((writers, LANES), 0)
+    rows_k = iota((2 * n_gy, LANES), 0)
+    rows_s = iota(square, 0)
+    rows_r = iota((most, LANES), 0)
+    lane = iota((1, LANES), 1)
+    f32, bf16 = jnp.float32, jnp.bfloat16
+    across = (((1,), (1,)), ((), ()))
+    count = jnp.zeros((writers, 1), f32)
+    kinds = jnp.zeros((2 * n_gy, 1), f32)
+    blocks_high = jnp.zeros((2 * n_gy, most), f32)
+    blocks_low = jnp.zeros((2 * n_gy, most), f32)
+    codes_high = jnp.zeros((writers, LANES), f32)
+    codes_low = jnp.zeros((writers, LANES), f32)
+
+    def numbers(where, number):
+        high = jnp.where(where, (number // 64).astype(f32), 0.0).astype(bf16)
+        low = jnp.where(where, (number % 64).astype(f32), 0.0).astype(bf16)
+        return high, low
+
+    def summed(a, b):
+        return lax.dot_general(a, b, across, preferred_element_type=f32)
+
+    for group in range(groups):
+        dest = dest_ref[pl.ds(group, 1), :]
+        lens = lens_ref[pl.ds(group, 1), :]
+        plane = dest % n_gy
+        short = jnp.where(lens <= LANES // 2, 1, 0)
+        one = (rows_w == plane * n_gx + dest // n_gy).astype(f32)
+        one_b = one.astype(bf16)
+        slot = jnp.sum(one * (dot(one_b, upper) + count), axis=0, keepdims=True).astype(jnp.int32)
+        count += jnp.sum(one, axis=1, keepdims=True)
+        kind = (rows_k == plane + n_gy * short).astype(f32)
+        place = jnp.sum(kind * (dot(kind.astype(bf16), upper) + kinds), axis=0, keepdims=True)
+        place = place.astype(jnp.int32)
+        kinds += jnp.sum(kind, axis=1, keepdims=True)
+        half = short * (place % 2)
+        row = jnp.where(short == 1, most - 1 - place // 2, place)
+        chosen = (rows_k == plane + n_gy * half).astype(bf16)
+        high, low = numbers(rows_r == row, turned_row(lane) + (group * LANES + 1))
+        blocks_high += summed(chosen, high)
+        blocks_low += summed(chosen, low)
+        high, low = numbers(rows_s == slot, row + 1 + 1024 * (short + half))
+        codes_high += summed(one_b, high)
+        codes_low += summed(one_b, low)
+        spread = jnp.where(diagonal, jnp.broadcast_to(lens.astype(f32), square), 0.0).astype(bf16)
+        keep_ref[pl.ds(group * LANES, LANES), :] = (freqs < dot(spread, ones)).astype(f32)
+    block = (blocks_high * 64.0 + blocks_low).astype(jnp.int32)
+    block = jnp.clip(jnp.where(block == 0, nblk, block - 1), 0, nblk)
+    first_ref[...] = block[:n_gy]
+    second_ref[...] = block[n_gy:]
+    code = (codes_high * 64.0 + codes_low).astype(jnp.int32)
+    where = jnp.where(code == 0, 3 * most, code // 1024 * most + code % 1024 - 1)
+    codes_ref[...] = jnp.clip(where, 0, 3 * most).reshape(n_gy, n_gx, LANES)
+    return jnp.where(2.0 * kinds[:n_gy] + kinds[n_gy:] > 2.0 * most, 1.0, 0.0)
+
+
 def exchange_kernel(
     sizes, field, dest, lens, table, result,
     x_in, y_out, y_in, z_out, z_in, turned, coeffs, rows, received, keep, slots_v, slots,
@@ -347,6 +412,390 @@
         pltpu.make_async_copy(received.at[c], result.at[c], out_sem.at[c]).wait()
 
 
+def relay_kernel(
+    sizes, field, dest, lens, table, result, flag,
+    x_in, y_out, y_in, z_out, z_in, turned, coeffs, shifted, packed, landed, spread, rows, received, keep,
+    first_v, second_v, first, second, codes_out, codes_in, codes,
+    part, parts, plane_sum, plane_sums,
+    halo_send, halo_recv, row_send, row_recv, own_sem, out_sem, slot_sem,
+    pack_send, pack_recv, code_send, code_recv,
+    part_send, part_recv, sum_send, sum_recv,
+):
+    n_gx, n_gy, n_wa, cells_x, cells_y, nblk, cap, most = sizes
+    writers = n_gx * n_gy
+    tiles_y = cells_y // 8
+    gx, gy, wa = lax.axis_index("gx"), lax.axis_index("gy"), lax.axis_index("wa")
+    me = gx * n_gy + gy
+
+    def writer(w):
+        return (w // n_gy, lax.rem(w, n_gy), wa)
+
+    barrier = pltpu.get_barrier_semaphore()
+
+    def greet(i, carry):
+        pl.semaphore_signal(
+            barrier, inc=1, device_id=writer(lax.rem(me + i, writers)), device_id_type=MESH
+        )
+        return carry
+
+    lax.fori_loop(1, writers, greet, 0)
+    for k in range(1, n_wa):
+        pl.semaphore_signal(
+            barrier, inc=1, device_id=(gx, gy, lax.rem(wa + k, n_wa)), device_id_type=MESH
+        )
+
+    lane = iota((8, LANES), 1)
+    sub = iota((8, LANES), 0)
+    zero = jnp.zeros((8, LANES), jnp.float32)
+    packs = cells_x * 8 // LANES
+    per = cells_x // packs
+
+    def tile(c, x, y):
+        return field[c, pl.ds(x * cells_y + y, tiles_y, stride=8), :]
+
+    def pack_y(c, j):
+        def pack(x, carry):
+            y_out[0, j, pl.ds(x, 1), :] = field[c, pl.ds(x * cells_y, 1), :]
+            y_out[1, j, pl.ds(x, 1), :] = field[c, pl.ds((x + 1) * cells_y - 1, 1), :]
+            return carry
+
+        lax.fori_loop(0, cells_x, pack, 0)
+
+    def pack_z(c, j):
+        for g in range(packs):
+
+            def pack(step, carry):
+                low, high = carry
+                for x, y in [(x, y) for x in range(2) for y in range(8)]:
+                    k = (step * 2 + x) * 8 + y
+                    here = tile(c, g * per + step * 2 + x, y)
+                    low = jnp.where(lane == k, pltpu.roll(here, k, 1), low)
+                    high = jnp.where(lane == k, pltpu.roll(here, lax.rem(k + 1, LANES), 1), high)
+                return low, high
+
+            low, high = lax.fori_loop(0, per // 2, pack, (zero, zero))
+            z_out[0, j, g] = low
+            z_out[1, j, g] = high
+
+    x_up = (lax.rem(gx + 1, n_gx), gy, wa)
+    x_down = (lax.rem(gx + n_gx - 1, n_gx), gy, wa)
+    y_up = (gx, lax.rem(gy + 1, n_gy), wa)
+    y_down = (gx, lax.rem(gy + n_gy - 1, n_gy), wa)
+    z_up = (gx, gy, lax.rem(wa + 1, n_wa))
+    z_down = (gx, gy, lax.rem(wa + n_wa - 1, n_wa))
+    faces = [
+        (z_out.at[0, 1], z_in.at[0, 1], z_down),
+        (z_out.at[1, 1], z_in.at[1, 1], z_up),
+        (y_out.at[0, 1], y_in.at[0, 1], y_down),
+        (y_out.at[1, 1], y_in.at[1, 1], y_up),
+        (z_out.at[0, 0], z_in.at[0, 0], z_down),
+        (z_out.at[1, 0], z_in.at[1, 0], z_up),
+        (y_out.at[0, 0], y_in.at[0, 0], y_down),
+        (y_out.at[1, 0], y_in.at[1, 0], y_up),
+        (field.at[pl.ds(1, 2), pl.ds(0, cells_y)], x_in.at[0], x_down),
+        (field.at[pl.ds(1, 2), pl.ds((cells_x - 1) * cells_y, cells_y)], x_in.at[1], x_up),
+    ]
+    halos = [
+        pltpu.make_async_remote_copy(
+            src_ref=source, dst_ref=target, send_sem=halo_send.at[k], recv_sem=halo_recv.at[k],
+            device_id=peer, device_id_type=MESH,
+        )
+        for k, (source, target, peer) in enumerate(faces)
+    ]
+
+    pack_z(1, 1)
+    pack_y(2, 1)
+    pack_z(0, 0)
+    pack_y(0, 0)
+    over = make_packing(n_gx, n_gy, most, dest, lens, first_v, second_v, codes_out, keep)
+    tables = [
+        pltpu.make_async_copy(first_v, first, slot_sem.at[0]),
+        pltpu.make_async_copy(second_v, second, slot_sem.at[1]),
+    ]
+    for copy in tables:
+        copy.start()
+    pl.semaphore_wait(barrier, writers - 1 + n_wa - 1)
+    for halo in halos:
+        halo.start()
+
+    def offset(k):
+        odd = lax.rem(k, 2)
+        return lax.rem(odd * ((k + 1) // 2) + (1 - odd) * (n_gy - k // 2), n_gy)
+
+    def plane_to(k):
+        return lax.rem(gy + offset(k), n_gy)
+
+    def plane_from(k):
+        return lax.rem(gy + n_gy - offset(k), n_gy)
+
+    def code_copy(k, slot):
+        return pltpu.make_async_remote_copy(
+            src_ref=codes_out.at[plane_to(k)], dst_ref=codes_in.at[slot], send_sem=code_send.at[k],
+            recv_sem=code_recv.at[k], device_id=(gx, plane_to(k), wa), device_id_type=MESH,
+        )
+
+    for k in range(1, n_gy):
+        code_copy(k, gy).start()
+    codes_in[pl.ds(gy, 1)] = codes_out[pl.ds(gy, 1)]
+    coeffs[pl.ds(nblk, 8), :] = zero
+    shifted[pl.ds(nblk, 8), :] = zero
+    spread[pl.ds(3 * most, 8), :] = zero
+
+    group = lane // BZ
+
+    def turn(tiles):
+        for step in (4, 2, 1):
+            bit = (group // step) % 2 == 1
+            out = list(tiles)
+            for a in range(8):
+                if a & step == 0:
+                    b = a | step
+                    out[a] = jnp.where(bit, pltpu.roll(tiles[b], BZ * step, 1), tiles[a])
+                    out[b] = jnp.where(bit, tiles[b], pltpu.roll(tiles[a], LANES - BZ * step, 1))
+            tiles = out
+        return tiles
+
+    def along_x(c, x, edge):
+        def near(at, d):
+            if edge == d:
+                return [x_in[d, c - 1, pl.ds(y, tiles_y, stride=8), :] for y in range(8)]
+            return [tile(c, at, y) for y in range(8)]
+
+        return [a - b for a, b in zip(near(x + 1, 0), near(x - 1, 1))]
+
+    def along_y(c, j, x):
+        here = [tile(c, x, y) for y in range(8)]
+        after = jnp.where(sub == tiles_y - 1, y_in[0, j, pl.ds(x, 1), :], pltpu.roll(here[0], tiles_y - 1, 0))
+        before = jnp.where(sub == 0, y_in[1, j, pl.ds(x, 1), :], pltpu.roll(here[7], 1, 0))
+        return [a - b for a, b in zip(here[1:] + [after], [before] + here[:-1])]
+
+    def along_z(c, j, x):
+        nexts, lasts = z_in[0, j, x // per], z_in[1, j, x // per]
+        out = []
+        for y in range(8):
+            k = lax.rem(x, per) * 8 + y
+            here = tile(c, x, y)
+            after = jnp.where(
+                lane == LANES - 1, pltpu.roll(nexts, LANES - 1 - k, 1), pltpu.roll(here, LANES - 1, 1)
+            )
+            before = jnp.where(
+                lane == 0, pltpu.roll(lasts, lax.rem(LANES - k, LANES), 1), pltpu.roll(here, 1, 1)
+            )
+            out.append(after - before)
+        return out
+
+    def curl(c, square):
+        def at(x, square, edge=None):
+            if c == 0:
+                pairs = zip(along_y(2, 1, x), along_z(1, 1, x))
+            elif c == 1:
+                pairs = zip(along_z(0, 0, x), along_x(2, x, edge))
+            else:
+                pairs = zip(along_x(1, x, edge), along_y(0, 0, x))
+            tiles = [(a - b) * 0.5 for a, b in pairs]
+            for t in tiles:
+                square += t * t
+            for z, t in enumerate(turn(tiles)):
+                turned[c, pl.ds(x * cells_y + z * tiles_y, tiles_y), :] = t
+            return square
+
+        if c == 0:
+            return lax.fori_loop(0, cells_x // 2, lambda i, q: at(2 * i + 1, at(2 * i, q)), square)
+        square = at(0, square, 1)
+        square = lax.fori_loop(1, cells_x - 1, at, square)
+        return at(cells_x - 1, square, 0)
+
+    chunk = 2 * LANES
+
+    def row_copy(c, k, e, slot):
+        column = lax.rem(gx + e, n_gx)
+        return pltpu.make_async_remote_copy(
+            src_ref=rows.at[c, column, plane_from(k)], dst_ref=received.at[c, slot],
+            send_sem=row_send.at[c, k, e], recv_sem=row_recv.at[c, k, e],
+            device_id=(column, gy, wa), device_id_type=MESH,
+        )
+
+    def own_copy(c, k):
+        plane = plane_from(k)
+        return pltpu.make_async_copy(
+            rows.at[c, gx, plane], received.at[c, gx * n_gy + plane], own_sem.at[c, k]
+        )
+
+    def pack_copy(c, k, slot):
+        return pltpu.make_async_remote_copy(
+            src_ref=packed.at[c, plane_to(k)], dst_ref=landed.at[c, slot],
+            send_sem=pack_send.at[c, k], recv_sem=pack_recv.at[c, k],
+            device_id=(gx, plane_to(k), wa), device_id_type=MESH,
+        )
+
+    def deliver(c):
+        def transform(k, carry):
+            at = pl.ds(k * chunk, chunk)
+            high, low = split(turned[c, at, :])
+            value = dot(high, table[0]) + (dot(low, table[0]) + dot(high, table[1]))
+            value = value * keep[at, :]
+            coeffs[at, :] = value
+            shifted[at, :] = pltpu.roll(value, LANES // 2, 1)
+            return carry
+
+        lax.fori_loop(0, nblk // chunk, transform, 0)
+
+        def fill(plane, q):
+            for s in range(64):
+                r = q * 64 + s
+                packed[c, plane, pl.ds(r, 1), :] = (
+                    coeffs[pl.ds(first[plane, r], 1), :] + shifted[pl.ds(second[plane, r], 1), :]
+                )
+
+        def rest(plane):
+            lax.fori_loop(1, most // 64, lambda q, carry: (fill(plane, q), carry)[1], 0)
+
+        fill(plane_to(1), 0)
+        rest(plane_to(1))
+
+        def step(k, carry):
+            fill(plane_to(k), 0)
+            pack_copy(c, k - 1, gy).start()
+            rest(plane_to(k))
+            return carry
+
+        lax.fori_loop(2, n_gy, step, 0)
+        fill(gy, 0)
+        pack_copy(c, n_gy - 1, gy).start()
+        rest(gy)
+
+    column64 = iota((64, LANES), 1) < LANES // 2
+
+    def pass_on(c, k, source):
+        def ready(q, carry):
+            full = source(q)
+            spread[pl.ds(q * 64, 64), :] = full
+            spread[pl.ds(most + q * 64, 64), :] = jnp.where(column64, full, 0.0)
+            turned_half = pltpu.roll(full, LANES // 2, 1)
+            spread[pl.ds(2 * most + q * 64, 64), :] = jnp.where(column64, turned_half, 0.0)
+            return carry
+
+        lax.fori_loop(0, most // 64, ready, 0)
+        plane = plane_from(k)
+
+        def gather(e):
+            column = lax.rem(gx + e, n_gx)
+            for s in range(cap):
+                rows[c, column, plane, pl.ds(s, 1), :] = spread[pl.ds(codes[plane, column, s], 1), :]
+
+        gather(1)
+
+        def step(e, carry):
+            gather(e)
+            row_copy(c, k, e - 1, gx * n_gy + plane).start()
+            return carry
+
+        lax.fori_loop(2, n_gx, step, 0)
+        gather(0)
+        row_copy(c, k, n_gx - 1, gx * n_gy + plane).start()
+        own_copy(c, k).start()
+
+    def relay(c):
+        pass_on(c, 0, lambda q: packed[c, gy, pl.ds(q * 64, 64), :])
+
+        def step(k, carry):
+            plane = plane_from(k)
+            pack_copy(c, k, plane).wait()
+            pass_on(c, k, lambda q: landed[c, plane, pl.ds(q * 64, 64), :])
+            return carry
+
+        lax.fori_loop(1, n_gy, step, 0)
+
+    def part_copy(i, slot):
+        return pltpu.make_async_remote_copy(
+            src_ref=part, dst_ref=parts.at[slot], send_sem=part_send.at[i],
+            recv_sem=part_recv.at[i], device_id=writer(lax.rem(me + i, writers)),
+            device_id_type=MESH,
+        )
+
+    def sum_copy(k, slot):
+        return pltpu.make_async_remote_copy(
+            src_ref=plane_sum, dst_ref=plane_sums.at[slot], send_sem=sum_send.at[k],
+            recv_sem=sum_recv.at[k], device_id=(gx, gy, lax.rem(wa + k, n_wa)),
+            device_id_type=MESH,
+        )
+
+    for halo in halos[:4]:
+        halo.wait()
+    square = curl(0, zero)
+    for copy in tables:
+        copy.wait()
+    deliver(0)
+    for halo in halos[4:]:
+        halo.wait()
+    square = curl(2, curl(1, square))
+    part[0] = square
+    part[1] = jnp.broadcast_to(over, (8, LANES))
+    parts[pl.ds(me, 1)] = part[...][None]
+
+    def part_start(i, carry):
+        part_copy(i, me).start()
+        return carry
+
+    lax.fori_loop(1, writers, part_start, 0)
+    deliver(1)
+
+    for k in range(1, n_gy):
+        code_copy(k, plane_from(k)).wait()
+    code_load = pltpu.make_async_copy(codes_in, codes, slot_sem.at[2])
+    code_load.start()
+    code_load.wait()
+    relay(0)
+    deliver(2)
+
+    def part_wait(i, carry):
+        part_copy(i, lax.rem(me + writers - i, writers)).wait()
+        return carry
+
+    lax.fori_loop(1, writers, part_wait, 0)
+    plane_sum[...] = jnp.sum(parts[...], axis=0)
+    plane_sums[pl.ds(wa, 1)] = plane_sum[...][None]
+    for k in range(1, n_wa):
+        sum_copy(k, wa).start()
+    relay(1)
+    for k in range(1, n_wa):
+        sum_copy(k, lax.rem(wa + n_wa - k, n_wa)).wait()
+    total = jnp.sum(plane_sums[...], axis=0)
+    flag[...] = total[1]
+    total = total[0]
+    total = jnp.sum(jnp.sum(total, axis=0, keepdims=True), axis=1, keepdims=True)
+    every = COMP * cells_x * cells_y * LANES * writers * n_wa
+    scale = 1.0 / jnp.sqrt(total / every + 1e-06)
+    scale = jnp.broadcast_to(jnp.broadcast_to(scale, (1, LANES)), (cap, LANES))
+
+    def finish(c, slot):
+        received[c, slot] = received[c, slot] * scale
+        pltpu.make_async_copy(received.at[c, slot], result.at[c, slot], out_sem.at[c]).start()
+
+    def take(c):
+        def from_plane(k, carry):
+            plane = plane_from(k)
+            own_copy(c, k).wait()
+            finish(c, gx * n_gy + plane)
+
+            def from_column(e, carry):
+                slot = lax.rem(gx + n_gx - e, n_gx) * n_gy + plane
+                row_copy(c, k, e, slot).wait()
+                finish(c, slot)
+                return carry
+
+            return lax.fori_loop(1, n_gx, from_column, carry)
+
+        lax.fori_loop(0, n_gy, from_plane, 0)
+
+    take(0)
+    relay(2)
+    take(1)
+    take(2)
+    for c in range(COMP):
+        pltpu.make_async_copy(received.at[c], result.at[c], out_sem.at[c]).wait()
+
+
 def local(n_gx, n_gy, n_wa, velocity, lengths, destinations):
     comps, cells_x, cells_y, cells_z = velocity.shape
     nblk = lengths.size
@@ -360,7 +809,15 @@
     f32 = jnp.float32
     packs = cells_x * cells_y // 8 // LANES
     dma = pltpu.SemaphoreType.DMA
-    result = pl.pallas_call(
+    operands = (
+        velocity.reshape(comps, cells_x * cells_y, cells_z),
+        destinations.reshape(nblk // LANES, LANES),
+        lengths.reshape(nblk // LANES, LANES),
+        table,
+    )
+    most = n_gx * cap * 3 // 4
+    result_shape = jax.ShapeDtypeStruct((comps, writers, cap, LANES), f32)
+    direct = pl.pallas_call(
         functools.partial(exchange_kernel, sizes),
         out_shape=jax.ShapeDtypeStruct((comps, writers, cap, LANES), f32),
         in_specs=[whole, whole, whole, whole],
@@ -397,12 +854,60 @@
         compiler_params=pltpu.CompilerParams(
             collective_id=0, has_side_effects=True, vmem_limit_bytes=40 * 2**20
         ),
-    )(
-        velocity.reshape(comps, cells_x * cells_y, cells_z),
-        destinations.reshape(nblk // LANES, LANES),
-        lengths.reshape(nblk // LANES, LANES),
-        table,
     )
+    relay = pl.pallas_call(
+        functools.partial(relay_kernel, sizes + (most,)),
+        out_shape=(result_shape, jax.ShapeDtypeStruct((8, LANES), f32)),
+        in_specs=[whole, whole, whole, whole],
+        out_specs=(pl.BlockSpec(memory_space=pl.ANY), whole),
+        scratch_shapes=[
+            pltpu.VMEM((2, 2, cells_y, LANES), f32),
+            pltpu.VMEM((2, 2, cells_x, LANES), f32),
+            pltpu.VMEM((2, 2, cells_x, LANES), f32),
+            pltpu.VMEM((2, 2, packs, 8, LANES), f32),
+            pltpu.VMEM((2, 2, packs, 8, LANES), f32),
+            pltpu.VMEM((comps, nblk, LANES), f32),
+            pltpu.VMEM((nblk + 8, LANES), f32),
+            pltpu.VMEM((nblk + 8, LANES), f32),
+            pltpu.VMEM((comps, n_gy, most, LANES), f32),
+            pltpu.VMEM((comps, n_gy, most, LANES), f32),
+            pltpu.VMEM((3 * most + 8, LANES), f32),
+            pltpu.VMEM((comps, n_gx, n_gy, cap, LANES), f32),
+            pltpu.VMEM((comps, writers, cap, LANES), f32),
+            pltpu.VMEM((nblk, LANES), f32),
+            pltpu.VMEM((n_gy, most), jnp.int32),
+            pltpu.VMEM((n_gy, most), jnp.int32),
+            pltpu.SMEM((n_gy, most), jnp.int32),
+            pltpu.SMEM((n_gy, most), jnp.int32),
+            pltpu.VMEM((n_gy, n_gx, LANES), jnp.int32),
+            pltpu.VMEM((n_gy, n_gx, LANES), jnp.int32),
+            pltpu.SMEM((n_gy, n_gx, LANES), jnp.int32),
+            pltpu.VMEM((2, 8, LANES), f32),
+            pltpu.VMEM((writers, 2, 8, LANES), f32),
+            pltpu.VMEM((2, 8, LANES), f32),
+            pltpu.VMEM((n_wa, 2, 8, LANES), f32),
+            dma((10,)),
+            dma((10,)),
+            dma((comps, n_gy, n_gx)),
+            dma((comps, n_gy, n_gx)),
+            dma((comps, n_gy)),
+            dma((comps,)),
+            dma((3,)),
+            dma((comps, n_gy)),
+            dma((comps, n_gy)),
+            dma((n_gy,)),
+            dma((n_gy,)),
+            dma((writers,)),
+            dma((writers,)),
+            dma((n_wa,)),
+            dma((n_wa,)),
+        ],
+        compiler_params=pltpu.CompilerParams(
+            collective_id=1, has_side_effects=True, vmem_limit_bytes=46 * 2**20
+        ),
+    )
+    result, flag = relay(*operands)
+    result = lax.cond(jnp.sum(flag) > 0.0, lambda: direct(*operands), lambda: result)
     return result.reshape(1, 1, comps, writers, cap, LANES)
 
 

time: 180 us -> 167 us (0.928); the launches traced: 178 us -> 167 us
  Pallas kernels: 172 us -> 159 us
    pallas_call x1, Pallas kernels: 172 us -> 159 us  [local(): result, flag = relay(*operands)]
    unnamed x7 -> x1, local copies, waits for them, and re-layouts: 5.98 us -> 6.61 us
where the time goes in v3:
time: 167 us
  Pallas kernels  159 us (95%)
  local copies, waits for them, and re-layouts  6.8 us (4%)
    pallas_call x1, Pallas kernels, local(): result, flag = relay(*operands)  159 us
    unnamed x1, local copies, waits for them, and re-layouts  6.61 us

profile of v3, /device:TPU:1, one launch (start us, length us, event | category | flops | bytes accessed | tf_op | source)
XLA Modules:
  0.0 167.4 jit_solution(14597089503771781327)
XLA Ops:
  0.1 0.1 multiply_select_fusion.1
  0.2 0.1 multiply_select_fusion
  0.3 0.1 broadcast_multiply_fusion
  0.4 0.2 mul.133
  0.6 158.7 %shard_map.39 = (f32[3,64,64,128]{3,2,1,0:T(8,128)}, f32[8,128]{1,0:T(8,128)S(1)}) custom-call(f32[3,2048,128]{2,1,0:T(8,128)} %bitcast.20, s32[16,128]{1,0:T(8,128)} %bitcast.24, s32[16,128]{1,0:T(8,128)} %bitcast.26, bf16[2,128,128]{2,1,0:T(8,128)(2,1)S(1)} %pad_maximum_fusion.table), custom_call_target="tpu_custom_call" | custom-call | tf_op jit(solution)/shard_map/pallas_call | solution.py:909
  159.3 0.6 reduce_sum.9
  160.5 0.2 conditional.1
  160.7 6.6 %copy.10 = f32[1,1,3,64,64,128]{5,4,3,2,1,0:T(8,128)} copy(f32[1,1,3,64,64,128]{5,4,3,2,1,0:T(8,128)} %get-tuple-element.27) | data formatting | bytes 12582912
  (6 shorter events, 0.1 us)
